TPU v7x, 256 devices: a whole 4x4x8 slice. The times are simulated.
256 devices in a mesh: grp: 8 (over y, core), dev: 32 (over x, z).
Axes of the slice: x: 4, y: 4, z: 8, core: 2. Of those that a mesh axis runs over, the one named last changes fastest.
Arguments:
- densities: bfloat16 [256, 200, 200], P(('grp', 'dev')), may hold values from -0.4375 to 0.4375
- core_hamiltonian: bfloat16 [256, 200, 200], P(('grp', 'dev')), may hold values from -0.21875 to 0.21875
- embedding: bfloat16 [256, 200, 200], P(('grp', 'dev')), may hold values from -0.21875 to 0.21875
- fit_factors: bfloat16 [768, 200, 200], P('dev'), may hold values from -0.059814453 to 0.059814453
- orthogonalizers: bfloat16 [256, 200, 200], P(('grp', 'dev'))
- pairs: int32 [3072, 2], replicated, may hold values from 0 to 255, as said below
- assignment: int32 [3072], replicated, may hold values from 0 to 31, as said below
- owner_map: int32 [256], replicated, may hold values from 0 to 255, as said below
Outputs:
- slot_energies: float32 [6144], P(('grp', 'dev'))
- total: float32 [], replicated
Inputs may be any that keep to these rules, and one draw needn't show every extreme that they name: `pairs`: dimer k belongs to group g = k // 384; its first fragment lies in block g, the fragments g * 32 to (g + 1) * 32 - 1, and its second fragment, different from the first, lies in block g or block g + 1 (only block g for the last group). `assignment`: no device receives more than 24 dimers of its group, and in every group some device receives exactly 24. `owner_map`: A permutation of the fragments that maps each block of 32 fragments onto the rows of the same block.
All inputs are finite; a program needn't handle non-finite values.
Results may differ from a plain program's by a relative error of at most 0.0003.
Values may be sent and summed in bfloat16 or wider, within the bound.
No kernel may reach another device: no remote copies, remote signals or barrier semaphores. Data moves between devices by JAX's collectives and lax.ppermute only.
A program may use at most 128 MiB of HBM per device.

v0:
```python
import jax
import jax.numpy as jnp
from jax import lax
from jax.sharding import Mesh
from jax.sharding import PartitionSpec as P

DIM_DEV = 12
SLOTS = 24
DEV = ("dev_0", "dev_1")
GRP_DEV = ("grp", "dev_0", "dev_1")
HALF_WIDTH = 4.0


def laid_out(tiles, dim):
    tiles = jnp.moveaxis(tiles, 0, dim)
    shape = tiles.shape
    return tiles.reshape(*shape[:dim], shape[dim] * shape[dim + 1], *shape[dim + 2 :])


def stacked_from(array, axes, order):
    tiles = array[None]
    for k in order:
        tiles = lax.all_gather(tiles, axes[k], axis=0, tiled=True)
    carried = [lax.axis_size(axes[k]) for k in reversed(order)]
    tiles = tiles.reshape(*carried, *array.shape)
    turned = sorted(range(len(order)), key=lambda place: order[len(order) - 1 - place])
    return tiles.transpose(*turned, *range(len(order), tiles.ndim)).reshape(-1, *array.shape)


def gathered_by_axis(array, axes, order, dim):
    return laid_out(stacked_from(array, axes, order), dim)


def summed_rows(terms, axes):
    total = terms.astype(jnp.bfloat16)
    for axis in axes:
        total = lax.psum_scatter(total, axis, scatter_dimension=0, tiled=True)
    return total.astype(jnp.float32)


def from_behind(block, axis, distance):
    devices = range(lax.axis_size(axis))
    route = [(i - distance, i) for i in devices if i - distance in devices]
    return lax.ppermute(block, axis, route)


def sent_together(arrays, axis, dim, along):
    widths = [a.shape[along] for a in arrays]
    both = jnp.concatenate(arrays, axis=along)
    whole = lax.all_gather(both, axis, axis=dim, tiled=True)
    return tuple(jnp.split(whole, [sum(widths[:k]) for k in range(1, len(widths))], axis=along))


def sent_to_all(array, axis):
    copies = jnp.broadcast_to(array, (lax.axis_size(axis), *array.shape))
    return lax.all_to_all(copies, axis, split_axis=0, concat_axis=0, tiled=True)


def of_everyone(array, axis):
    return sent_to_all(array, axis).sum(axis=0)


def product(left, right):
    return jnp.dot(left, right, preferred_element_type=jnp.float32)


def dimer_energy(fock_i, fock_j, dens_i, dens_j, ortho_i, ortho_j):
    coupling = (0.5 * (product(fock_i, dens_j) + product(dens_i, fock_j))).astype(jnp.bfloat16)
    upper_left = product(fock_i, ortho_i).astype(jnp.bfloat16)
    upper_right = product(coupling, ortho_j).astype(jnp.bfloat16)
    lower_left = product(coupling.T, ortho_i).astype(jnp.bfloat16)
    lower_right = product(fock_j, ortho_j).astype(jnp.bfloat16)
    top_rows = jnp.concatenate(
        [product(ortho_i.T, upper_left), product(ortho_i.T, upper_right)], axis=1
    )
    bottom_rows = jnp.concatenate(
        [product(ortho_j.T, lower_left), product(ortho_j.T, lower_right)], axis=1
    )
    ortho_fock = jnp.concatenate([top_rows, bottom_rows], axis=0)
    size_two = ortho_fock.shape[0]
    half_basis = fock_i.shape[0]
    start = (0.5 * jnp.eye(size_two, dtype=jnp.float32) - ortho_fock / (2.0 * HALF_WIDTH)).astype(
        jnp.bfloat16
    )
    square = product(start, start).astype(jnp.bfloat16)
    cube = product(square, start)
    purified = (3.0 * square.astype(jnp.float32) - 2.0 * cube).astype(jnp.bfloat16)
    left_part = jnp.concatenate(
        [product(ortho_i, purified[:half_basis]), product(ortho_j, purified[half_basis:])], axis=0
    ).astype(jnp.bfloat16)
    new_density = jnp.concatenate(
        [
            product(left_part[:, :half_basis], ortho_i.T),
            product(left_part[:, half_basis:], ortho_j.T),
        ],
        axis=1,
    )
    fock_top = jnp.concatenate([fock_i, coupling], axis=1)
    fock_bottom = jnp.concatenate([coupling.T, fock_j], axis=1)
    dimer_fock = jnp.concatenate([fock_top, fock_bottom], axis=0).astype(jnp.float32)
    monomer_i = jnp.sum(dens_i.astype(jnp.float32) * fock_i.astype(jnp.float32))
    monomer_j = jnp.sum(dens_j.astype(jnp.float32) * fock_j.astype(jnp.float32))
    return jnp.sum(new_density * dimer_fock) - monomer_i - monomer_j


def on_device(
    densities,
    core_hamiltonian,
    embedding,
    fit_factors,
    orthogonalizers,
    pairs,
    assignment,
    owner_map,
):
    members = lax.axis_size(DEV)
    group_index = lax.axis_index("grp")
    member_index = lax.axis_index(DEV)
    basis_size = densities.shape[1]
    aux_count = fit_factors.shape[0]
    flat_fit = fit_factors.reshape(aux_count, basis_size * basis_size)
    gathered = gathered_by_axis(densities, DEV, (0, 1), 0)
    flat_dens = gathered.reshape(members, basis_size * basis_size)
    coeffs = lax.dot_general(
        flat_dens, flat_fit, (((1,), (1,)), ((), ())), preferred_element_type=jnp.float32
    ).astype(jnp.bfloat16)
    coulomb = summed_rows(
        jnp.dot(coeffs, flat_fit, preferred_element_type=jnp.float32).reshape(
            densities.shape[0] * lax.axis_size(DEV), basis_size, basis_size
        ),
        DEV,
    )
    fock_rows = (
        core_hamiltonian.astype(jnp.float32) + embedding.astype(jnp.float32) + coulomb
    ).astype(jnp.bfloat16)
    local_pair = jnp.stack([fock_rows, orthogonalizers], axis=1)
    monomer = jnp.stack([fock_rows, densities, orthogonalizers], axis=1)
    following = from_behind(monomer, "grp", -1)
    own_pair, next_pool = sent_together((local_pair, following), DEV, 0, 1)
    dim_group = DIM_DEV * members
    group_pairs = lax.dynamic_slice_in_dim(pairs, group_index * dim_group, dim_group, 0)
    group_assign = lax.dynamic_slice_in_dim(assignment, group_index * dim_group, dim_group, 0)
    is_mine = group_assign == member_index
    mine_count = is_mine.astype(jnp.int32)
    before = jnp.cumsum(mine_count) - mine_count
    select = is_mine[None, :] & (before[None, :] == jnp.arange(SLOTS, dtype=jnp.int32)[:, None])
    list_positions = jnp.arange(dim_group, dtype=jnp.int32)

    def energy_of(listed):
        pair_ids = group_pairs[listed]
        first_row = owner_map[pair_ids[0]] - group_index * members
        second_row = owner_map[pair_ids[1]] - group_index * members
        in_next = second_row >= members
        pool_row = jnp.where(in_next, second_row - members, second_row)
        first_pair = own_pair[first_row]
        own_second = own_pair[pool_row]
        next_second = next_pool[pool_row]
        second_fock = jnp.where(in_next, next_second[0], own_second[0])
        second_dens = jnp.where(in_next, next_second[1], gathered[pool_row])
        second_ortho = jnp.where(in_next, next_second[2], own_second[1])
        return dimer_energy(
            first_pair[0],
            second_fock,
            gathered[first_row],
            second_dens,
            first_pair[1],
            second_ortho,
        )

    listed = member_index * DIM_DEV + jnp.arange(DIM_DEV, dtype=jnp.int32)
    values = lax.map(energy_of, listed)
    spread = jnp.sum(
        jnp.where(list_positions[None, :] == listed[:, None], values[:, None], 0.0), axis=0
    )
    group_values = of_everyone(spread, DEV)
    slot_energies = jnp.sum(jnp.where(select, group_values[None, :], 0.0), axis=1)
    energy_sum = of_everyone(jnp.sum(group_values), "grp")
    return (slot_energies, energy_sum)


def solution(mesh):
    torus = Mesh(mesh.devices.reshape(mesh.shape["grp"], 4, 8), ("grp", "dev_0", "dev_1"))
    in_specs = (
        P(GRP_DEV, None, None),
        P(GRP_DEV, None, None),
        P(GRP_DEV, None, None),
        P(DEV, None, None),
        P(GRP_DEV, None, None),
        P(),
        P(),
        P(),
    )
    out_specs = (P(GRP_DEV), P())
    return jax.shard_map(
        on_device, mesh=torus, in_specs=in_specs, out_specs=out_specs, check_vma=False
    )
```

profile of v0, /device:TPU:1, one launch (start us, length us, event | category | flops | bytes accessed | tf_op | source)
XLA Modules:
  0.0 740.4 jit_solution(16473954267569400295)
XLA Ops:
  7.2 12.8 %all-gather = bf16[4,200,200]{2,1,0:T(8,128)(2,1)} all-gather(bf16[1,200,200]{2,1,0:T(8,128)(2,1)} %param.10), channel_id=2, replica_groups=mesh['grp'=8,'dev_0'=4,'dev_1'=8] {'dev_0'}, dimensions={0}, use_global_device_ids=true | all-gather | bytes 400000 | tf_op jit(solution)/shard_map/all_gather | solution.py:23
  20.1 3.9 reshape.83
  24.1 5.0 dot_general.108
  29.1 41.3 %all-gather.7.cloned.1.call-done = bf16[32,200,200]{2,1,0:T(8,128)(2,1)} async-done(((bf16[4,200,200]{2,1,0:T(8,128)(2,1)}), bf16[32,200,200]{2,1,0:T(8,128)(2,1)}) %all-gather.7.cloned.1.call-update) | async-done | bytes 2560016 | tf_op jit(solution)/shard_map/all_gather | solution.py:23
  70.4 2.1 copy.62
  72.6 4.1 reshape_reshape_reshape.3
  76.6 8.2 %fusion.41 = bf16[32,200,200]{2,0,1:T(8,128)(2,1)} fusion(bf16[200,200,24]{1,0,2:T(8,128)(2,1)} %dot_general.108, bf16[32,40000]{1,0:T(8,128)(2,1)} %reshape_reshape_reshape.3, bf16[24,40000]{1,0:T(8,128)(2,1)} %copy-done.2), kind=kOutput, calls=%fused_computation.64 | convolution fusion | flops 124160768 | bytes 8960000 | tf_op jit(solution)/shard_map/dot_general | solution.py:128
  86.7 79.8 %all-reduce.3.cloned.1.call-done = bf16[32,200,200]{2,0,1:T(8,128)(2,1)} async-done(((bf16[32,200,200]{2,0,1:T(8,128)(2,1)}), bf16[32,200,200]{2,0,1:T(8,128)(2,1)}) %all-reduce.3.cloned.1.call-update) | async-done | bytes 2560016
  168.8 33.8 %reduce-scatter.3.cloned.1.call-done = bf16[1,200,200]{2,1,0:T(8,128)(2,1)} async-done(((bf16[8,200,200]{2,1,0:T(8,128)(2,1)}), bf16[1,200,200]{2,1,0:T(8,128)(2,1)}) %reduce-scatter.3.cloned.1.call-update) | async-done | bytes 80016 | tf_op jit(solution)/shard_map/reduce_scatter | solution.py:37
  203.8 7.6 %collective-permute-start = (bf16[1,3,200,200]{3,2,1,0:T(8,128)(2,1)S(1)}, bf16[1,3,200,200]{3,2,1,0:T(8,128)(2,1)S(1)}, u32[]{:S(2)}, u32[]{:S(2)}) collective-permute-start(bf16[1,3,200,200]{3,2,1,0:T(8,128)(2,1)S(1)} %pad_maximum_fusion.3), channel_id=1, source_target_pairs={{32,0},{64,32},{96,64},{128,96},{160,128},{192,160},{224,192},{33,... | collective-permute-start | bytes 720008 | tf_op jit(solution)/shard_map/ppermute | solution.py:44
  211.4 5.4 collective-permute-done
  219.1 4.0 copy.42
  223.1 130.0 %all-gather.5.cloned.1.call-done = bf16[32,5,200,200]{3,2,1,0:T(8,128)(2,1)} async-done(((bf16[1,5,200,200]{3,2,1,0:T(8,128)(2,1)}), bf16[32,5,200,200]{3,2,1,0:T(8,128)(2,1)}) %all-gather.5.cloned.1.call-update) | async-done | bytes 12800016 | tf_op jit(solution)/shard_map/all_gather | solution.py:50
  353.1 6.0 split.8
  359.1 10.3 %copy.43 = bf16[32,2,200,200]{2,3,1,0:T(8,128)(2,1)} copy(bf16[32,2,200,200]{3,2,1,0:T(8,128)(2,1)} %split.8) | data formatting | bytes 10240000 | tf_op jit(solution)/shard_map/while | solution.py:171
  369.3 8.2 %split.9 = bf16[32,3,200,200]{3,2,1,0:T(8,128)(2,1)} slice(bf16[32,5,200,200]{3,2,1,0:T(8,128)(2,1)} %all-gather.5.cloned.1.call-done), slice={[0:32], [2:5], [0:200], [0:200]} | slice | bytes 15360000 | tf_op jit(solution)/shard_map/split | solution.py:51
  377.5 327.1 %while.12 = (s32[]{:T(128)}, f32[12]{0:T(128)S(1)}, s32[12]{0:T(128)S(1)}, s32[384,2]{0,1:T(2,128)S(1)}, s32[256]{0:T(256)S(1)}, /*index=5*/s32[]{:T(128)}, bf16...) while((s32[]{:T(128)}, f32[12]{0:T(128)S(1)}, ...), condition=%wide.region_8.9_spmd, body=%wide.region_4.8_spmd.sunk | while | flops 550840000 | bytes 10055895 | solution.py:171
  388.9 1.8 multiply_reduce_fusion.3
  396.1 1.4 fusion.127
  416.2 1.8 multiply_reduce_fusion.3
  420.7 1.3 fusion.125
  423.4 1.4 fusion.127
  443.4 1.8 multiply_reduce_fusion.3
  448.0 1.3 fusion.125
  450.6 1.4 fusion.127
  470.7 1.8 multiply_reduce_fusion.3
  475.2 1.3 fusion.125
  477.9 1.4 fusion.127
  497.9 1.8 multiply_reduce_fusion.3
  505.2 1.4 fusion.127
  525.2 1.8 multiply_reduce_fusion.3
  532.4 1.4 fusion.127
  552.5 1.8 multiply_reduce_fusion.3
  559.7 1.4 fusion.127
  579.7 1.8 multiply_reduce_fusion.3
  586.9 1.4 fusion.127
  607.0 1.8 multiply_reduce_fusion.3
  614.2 1.4 fusion.127
  634.2 1.8 multiply_reduce_fusion.3
  641.5 1.4 fusion.127
  661.5 1.8 multiply_reduce_fusion.3
  668.7 1.4 fusion.127
  688.8 1.8 multiply_reduce_fusion.3
  696.0 1.4 fusion.127
  705.4 5.4 all-to-all-start
  710.8 8.7 %all-to-all-done = f32[32,1,384]{2,1,0:T(1,128)S(1)} async-done(((f32[32,1,384]{2,1,0:T(1,128)}), f32[32,1,384]{2,1,0:T(1,128)S(1)}, u32[]{:S(2)}, u32[]{:S(2)}) %all-to-all-start) | async-done | bytes 49184 | tf_op jit(solution)/shard_map/all_to_all | solution.py:56
  721.5 7.2 all-to-all-start.1
  729.3 4.0 all-to-all-done.1
  (316 shorter events, 185.6 us)
Async XLA Ops:
  7.2 211.8 %copy-start = (s32[3072,2]{0,1:T(2,128)S(1)}, s32[3072,2]{0,1:T(2,128)}, u32[]{:S(2)}) copy-start(s32[3072,2]{0,1:T(2,128)} %param.15) | copy-start | bytes 73732
  7.2 63.2 %all-gather.7.cloned.1.call-start = ((), (), s32[]{:S(2)}) async-start(), calls=%async_computation.5 | async-start | bytes 3686400 | tf_op jit(solution)/shard_map/all_gather | solution.py:23
  20.1 146.4 %all-reduce.3.cloned.1.call-start = ((), (), s32[]{:S(2)}) async-start(), calls=%async_computation.6 | async-start | bytes 6553600
  24.0 46.4 %copy-start.2 = (bf16[24,40000]{1,0:T(8,128)(2,1)}, bf16[24,40000]{1,0:T(8,128)(2,1)S(1)}, u32[]{:S(2)}) copy-start(bf16[24,40000]{1,0:T(8,128)(2,1)S(1)} %reshape.83) | copy-start | bytes 5760004
  84.8 0.7 copy-start.6
  84.8 118.9 %copy-start.3 = (bf16[1,200,200]{2,1,0:T(8,128)(2,1)S(1)}, bf16[1,200,200]{2,1,0:T(8,128)(2,1)}, u32[]{:S(2)}) copy-start(bf16[1,200,200]{2,1,0:T(8,128)(2,1)} %param.10) | copy-start | bytes 240004
  84.8 118.9 %copy-start.4 = (bf16[1,200,200]{2,1,0:T(8,128)(2,1)S(1)}, bf16[1,200,200]{2,1,0:T(8,128)(2,1)}, u32[]{:S(2)}) copy-start(bf16[1,200,200]{2,1,0:T(8,128)(2,1)} %param.14) | copy-start | bytes 240004
  84.8 117.8 %reduce-scatter.3.cloned.1.call-start = ((), (), s32[]{:S(2)}) async-start(), calls=%async_computation.3 | async-start | bytes 921600 | tf_op jit(solution)/shard_map/reduce_scatter | solution.py:37
  168.8 184.3 %all-gather.5.cloned.1.call-start = ((), (), s32[]{:S(2)}) async-start(), calls=%async_computation.4 | async-start | bytes 16896000 | tf_op jit(solution)/shard_map/all_gather | solution.py:50
  203.8 13.0 %collective-permute-start = (bf16[1,3,200,200]{3,2,1,0:T(8,128)(2,1)S(1)}, bf16[1,3,200,200]{3,2,1,0:T(8,128)(2,1)S(1)}, u32[]{:S(2)}, u32[]{:S(2)}) collective-permute-start(bf16[1,3,200,200]{3,2,1,0:T(8,128)(2,1)S(1)} %pad_maximum_fusion.3), channel_id=1, source_target_pairs={{32,0},{64,32},{96,64},{128,96},{160,128},{192,160},{224,192},{33,... | collective-permute-start | bytes 720008 | tf_op jit(solution)/shard_map/ppermute | solution.py:44
  369.3 8.2 %copy-start.5 = (s32[256]{0:T(256)S(1)}, s32[256]{0:T(256)}, u32[]{:S(2)}) copy-start(s32[256]{0:T(256)} %param.17) | copy-start | bytes 3076
  704.6 29.2 %copy-start.1 = (s32[3072,2]{0,1:T(2,128)S(1)}, s32[3072,2]{0,1:T(2,128)}, u32[]{:S(2)}) copy-start(s32[3072,2]{0,1:T(2,128)} %param.15) | copy-start | bytes 73732
  705.4 14.2 %all-to-all-start = ((f32[32,1,384]{2,1,0:T(1,128)}), f32[32,1,384]{2,1,0:T(1,128)S(1)}, u32[]{:S(2)}, u32[]{:S(2)}) async-start(f32[32,1,384]{2,1,0:T(1,128)} %broadcast_in_dim.50), calls=%async_computation.1 | async-start | bytes 98304 | tf_op jit(solution)/shard_map/all_to_all | solution.py:56
  721.5 11.8 %all-to-all-start.1 = ((f32[8,1,1]{2,1,0:T(1,128)}), f32[8,1,1]{2,1,0:T(1,128)S(1)}, u32[]{:S(2)}, u32[]{:S(2)}) async-start(f32[8,1,1]{2,1,0:T(1,128)} %broadcast_in_dim.53), calls=%async_computation.2 | async-start | bytes 8192 | tf_op jit(solution)/shard_map/all_to_all | solution.py:56
Sparse Core Ops, SparseCore 0:
  20.2 50.1 all-gather.6
  84.9 81.5 all-reduce.2
  169.0 33.5 reduce-scatter.2
  217.9 135.1 all-gather.4
where the time goes:
time: 746 us; the launch traced here: 740 us
  waiting for transfers between devices  303 us (41%)
  matrix products  140 us (19%)
  loops' own time  109 us (15%)
  local copies, waits for them, and re-layouts  91.6 us (12%)
  other arithmetic  49 us (7%)
  starting transfers between devices  20.3 us (3%)
  between operations  14.5 us (2%)
  blocking collectives  12.8 us (2%)
    dot_general x144, matrix products, product(): return jnp.dot(left, right, preferred_element_type=jnp.float32)  131 us
    all_gather x1, waiting for transfers between devices, sent_together(): whole = lax.all_gather(both, axis, axis=dim, tiled=True)  130 us
    another operation x1, loops' own time, on_device(): values = lax.map(energy_of, listed)  109 us
    unnamed x5, waiting for transfers between devices  79.9 us
    all_gather x1, waiting for transfers between devices, stacked_from(): tiles = lax.all_gather(tiles, axes[k], axis=0, tiled=True)  41.3 us
    reduce_scatter x1, waiting for transfers between devices, summed_rows(): total = lax.psum_scatter(total, axis, scatter_dimension=0, tiled=True)  33.8 us
    reduce_sum x12, other arithmetic, dimer_energy(): monomer_j = jnp.sum(dens_j.astype(jnp.float32) * fock_j.astype(jnp.float32))  22.1 us
  transfers between devices with their start and end apart: 7, of which 7 were waited for; matrix products, arithmetic and copies ran while one was open for 2% of the time, Pallas kernels for 0%

commit v1 on v0

--- a/solution.py
+++ b/solution.py
@@ -20,7 +20,13 @@
 def stacked_from(array, axes, order):
     tiles = array[None]
     for k in order:
-        tiles = lax.all_gather(tiles, axes[k], axis=0, tiled=True)
+        x_in = axes[k]
+        tiles = jnp.concatenate(
+            lax.all_to_all(
+                jnp.stack([tiles] * lax.axis_size(x_in)), x_in, split_axis=0, concat_axis=0
+            ),
+            0,
+        )
     carried = [lax.axis_size(axes[k]) for k in reversed(order)]
     tiles = tiles.reshape(*carried, *array.shape)
     turned = sorted(range(len(order)), key=lambda place: order[len(order) - 1 - place])

time: 746 us -> 779 us (1.044)
  waiting for transfers between devices: 303 us -> 325 us
  starting transfers between devices: 20.3 us -> 28.4 us
    all_to_all x0 -> x1, waiting for transfers between devices: none -> 68.1 us  [stacked_from(): lax.all_to_all(jnp.stack([tiles] * lax.axis_size(x_in)), x_in, split_axis...]
    all_gather x1 -> x0, waiting for transfers between devices: 41.3 us -> none  [stacked_from(): tiles = lax.all_gather(tiles, axes[k], axis=0, tiled=True)]
    all_gather x1 -> x0, blocking collectives: 12.8 us -> none  [stacked_from(): tiles = lax.all_gather(tiles, axes[k], axis=0, tiled=True)]
    all_to_all x0 -> x1, blocking collectives: none -> 11.9 us  [stacked_from(): lax.all_to_all(jnp.stack([tiles] * lax.axis_size(x_in)), x_in, split_axis...]
    all_to_all x0 -> x1, starting transfers between devices: none -> 8.19 us  [stacked_from(): lax.all_to_all(jnp.stack([tiles] * lax.axis_size(x_in)), x_in, split_axis...]
    unnamed x5 -> x4, waiting for transfers between devices: 79.9 us -> 75.5 us
where the time goes in v1:
time: 779 us; the launch traced here: 773 us
  waiting for transfers between devices  325 us (42%)
  matrix products  140 us (18%)
  loops' own time  109 us (14%)
  local copies, waits for them, and re-layouts  94.9 us (12%)
  other arithmetic  49 us (6%)
  starting transfers between devices  28.4 us (4%)
  between operations  14.5 us (2%)
  blocking collectives  11.9 us (2%)
    dot_general x144, matrix products, product(): return jnp.dot(left, right, preferred_element_type=jnp.float32)  131 us
    all_gather x1, waiting for transfers between devices, sent_together(): whole = lax.all_gather(both, axis, axis=dim, tiled=True)  130 us
    another operation x1, loops' own time, on_device(): values = lax.map(energy_of, listed)  109 us
    unnamed x4, waiting for transfers between devices  75.5 us
    all_to_all x1, waiting for transfers between devices, stacked_from(): lax.all_to_all(jnp.stack([tiles] * lax.axis_size(x_in)), x_in, split_axis...  68.1 us
    reduce_scatter x1, waiting for transfers between devices, summed_rows(): total = lax.psum_scatter(total, axis, scatter_dimension=0, tiled=True)  33.8 us
    reduce_sum x12, other arithmetic, dimer_energy(): monomer_j = jnp.sum(dens_j.astype(jnp.float32) * fock_j.astype(jnp.float32))  22.1 us
  transfers between devices with their start and end apart: 7, of which 7 were waited for; matrix products, arithmetic and copies ran while one was open for 2% of the time, Pallas kernels for 0%

profile of v1, /device:TPU:1, one launch (start us, length us, event | category | flops | bytes accessed | tf_op | source)
XLA Modules:
  0.0 772.8 jit_solution(11169452635058588679)
XLA Ops:
  8.1 11.9 %all_to_all.22 = bf16[4,1,1,200,200]{4,3,2,1,0:T(8,128)(2,1)S(1)} all-to-all(bf16[4,1,1,200,200]{4,3,2,1,0:T(8,128)(2,1)S(1)} %stack.20), channel_id=1, replica_groups=mesh['grp'=8,'dev_0'=4,'dev_1'=8] {'dev_0'}, dimensions={0} | all-to-all | bytes 640000 | tf_op jit(solution)/shard_map/all_to_all | solution.py:25
  20.0 1.9 stack.21
  21.9 8.2 %all-to-all-start.1 = ((bf16[8,4,1,200,200]{4,3,1,2,0:T(8,128)(2,1)}), bf16[8,4,1,200,200]{4,3,1,2,0:T(8,128)(2,1)}, u32[]{:S(2)}, u32[]{:S(2)}) async-start(bf16[8,4,1,200,200]{4,3,1,2,0:T(8,128)(2,1)} %stack.21), calls=%async_computation.1 | async-start | bytes 6553600 | tf_op jit(solution)/shard_map/all_to_all | solution.py:25
  30.1 3.9 reshape.86
  34.1 5.1 dot_general.108
  39.2 68.1 %all-to-all-done.1 = bf16[8,4,1,200,200]{4,3,1,2,0:T(8,128)(2,1)} async-done(((bf16[8,4,1,200,200]{4,3,1,2,0:T(8,128)(2,1)}), bf16[8,4,1,200,200]{4,3,1,2,0:T(8,128)(2,1)}, u32[]{:S(2)}, u32[]{:S(2)}) %all-to-all-start.1) | async-done | bytes 2560032 | tf_op jit(solution)/shard_map/all_to_all | solution.py:25
  107.2 2.1 copy.68
  109.4 4.1 reshape_reshape_reshape.3
  113.4 8.2 %fusion.41 = bf16[32,200,200]{2,0,1:T(8,128)(2,1)} fusion(bf16[200,200,24]{1,0,2:T(8,128)(2,1)} %dot_general.108, bf16[32,40000]{1,0:T(8,128)(2,1)} %reshape_reshape_reshape.3, bf16[24,40000]{1,0:T(8,128)(2,1)} %copy-done.2), kind=kOutput, calls=%fused_computation.63 | convolution fusion | flops 124160768 | bytes 8960000 | tf_op jit(solution)/shard_map/dot_general | solution.py:134
  123.5 75.5 %all-reduce.3.cloned.1.call-done = bf16[32,200,200]{2,0,1:T(8,128)(2,1)} async-done(((bf16[32,200,200]{2,0,1:T(8,128)(2,1)}), bf16[32,200,200]{2,0,1:T(8,128)(2,1)}) %all-reduce.3.cloned.1.call-update) | async-done | bytes 2560016
  201.3 33.8 %reduce-scatter.3.cloned.1.call-done = bf16[1,200,200]{2,1,0:T(8,128)(2,1)} async-done(((bf16[8,200,200]{2,1,0:T(8,128)(2,1)}), bf16[1,200,200]{2,1,0:T(8,128)(2,1)}) %reduce-scatter.3.cloned.1.call-update) | async-done | bytes 80016 | tf_op jit(solution)/shard_map/reduce_scatter | solution.py:43
  236.2 7.6 collective-permute-start
  243.8 5.4 collective-permute-done
  251.5 4.4 copy.49
  255.9 129.6 %all-gather.2.cloned.1.call-done = bf16[32,5,200,200]{3,2,1,0:T(8,128)(2,1)} async-done(((bf16[1,5,200,200]{3,2,1,0:T(8,128)(2,1)}), bf16[32,5,200,200]{3,2,1,0:T(8,128)(2,1)}) %all-gather.2.cloned.1.call-update) | async-done | bytes 12800016 | tf_op jit(solution)/shard_map/all_gather | solution.py:56
  385.5 6.0 split.8
  391.5 10.3 %copy.47 = bf16[32,2,200,200]{2,3,1,0:T(8,128)(2,1)} copy(bf16[32,2,200,200]{3,2,1,0:T(8,128)(2,1)} %split.8) | data formatting | bytes 10240000 | tf_op jit(solution)/shard_map/while | solution.py:177
  401.8 8.2 %split.9 = bf16[32,3,200,200]{3,2,1,0:T(8,128)(2,1)} slice(bf16[32,5,200,200]{3,2,1,0:T(8,128)(2,1)} %all-gather.2.cloned.1.call-done), slice={[0:32], [2:5], [0:200], [0:200]} | slice | bytes 15360000 | tf_op jit(solution)/shard_map/split | solution.py:57
  410.0 327.1 %while.12 = (s32[]{:T(128)}, f32[12]{0:T(128)S(1)}, s32[12]{0:T(128)S(1)}, s32[384,2]{0,1:T(2,128)S(1)}, s32[256]{0:T(256)S(1)}, /*index=5*/s32[]{:T(128)}, bf16...) while((s32[]{:T(128)}, f32[12]{0:T(128)S(1)}, ...), condition=%wide.region_8.9_spmd, body=%wide.region_4.8_spmd.sunk | while | flops 550840000 | bytes 10055895 | solution.py:177
  421.3 1.8 multiply_reduce_fusion.3
  425.9 1.3 fusion.126
  428.6 1.4 fusion.128
  448.6 1.8 multiply_reduce_fusion.3
  455.8 1.4 fusion.128
  475.9 1.8 multiply_reduce_fusion.3
  483.1 1.4 fusion.128
  503.1 1.8 multiply_reduce_fusion.3
  510.4 1.4 fusion.128
  530.4 1.8 multiply_reduce_fusion.3
  537.6 1.4 fusion.128
  557.6 1.8 multiply_reduce_fusion.3
  564.9 1.4 fusion.128
  584.9 1.8 multiply_reduce_fusion.3
  592.1 1.4 fusion.128
  612.2 1.8 multiply_reduce_fusion.3
  619.4 1.4 fusion.128
  639.4 1.8 multiply_reduce_fusion.3
  646.6 1.4 fusion.128
  666.7 1.8 multiply_reduce_fusion.3
  673.9 1.4 fusion.128
  693.9 1.8 multiply_reduce_fusion.3
  701.2 1.4 fusion.128
  721.2 1.8 multiply_reduce_fusion.3
  728.4 1.4 fusion.128
  737.8 5.4 all-to-all-start.2
  743.2 8.7 %all-to-all-done.2 = f32[32,1,384]{2,1,0:T(1,128)S(1)} async-done(((f32[32,1,384]{2,1,0:T(1,128)}), f32[32,1,384]{2,1,0:T(1,128)S(1)}, u32[]{:S(2)}, u32[]{:S(2)}) %all-to-all-start.2) | async-done | bytes 49184 | tf_op jit(solution)/shard_map/all_to_all | solution.py:62
  753.9 7.2 all-to-all-start.3
  761.7 4.0 all-to-all-done.3
  (317 shorter events, 189.2 us)
Async XLA Ops:
  7.2 244.2 %copy-start = (s32[3072,2]{0,1:T(2,128)S(1)}, s32[3072,2]{0,1:T(2,128)}, u32[]{:S(2)}) copy-start(s32[3072,2]{0,1:T(2,128)} %param.15) | copy-start | bytes 73732
  21.9 85.3 %all-to-all-start.1 = ((bf16[8,4,1,200,200]{4,3,1,2,0:T(8,128)(2,1)}), bf16[8,4,1,200,200]{4,3,1,2,0:T(8,128)(2,1)}, u32[]{:S(2)}, u32[]{:S(2)}) async-start(bf16[8,4,1,200,200]{4,3,1,2,0:T(8,128)(2,1)} %stack.21), calls=%async_computation.1 | async-start | bytes 6553600 | tf_op jit(solution)/shard_map/all_to_all | solution.py:25
  30.1 168.8 %all-reduce.3.cloned.1.call-start = ((), (), s32[]{:S(2)}) async-start(), calls=%async_computation.7 | async-start | bytes 6553600
  34.1 5.1 copy-start.2
  121.6 0.7 copy-start.6
  121.6 114.5 %copy-start.3 = (bf16[1,200,200]{2,1,0:T(8,128)(2,1)S(1)}, bf16[1,200,200]{2,1,0:T(8,128)(2,1)}, u32[]{:S(2)}) copy-start(bf16[1,200,200]{2,1,0:T(8,128)(2,1)} %param.10) | copy-start | bytes 240004
  121.6 114.5 %copy-start.4 = (bf16[1,200,200]{2,1,0:T(8,128)(2,1)S(1)}, bf16[1,200,200]{2,1,0:T(8,128)(2,1)}, u32[]{:S(2)}) copy-start(bf16[1,200,200]{2,1,0:T(8,128)(2,1)} %param.14) | copy-start | bytes 240004
  121.6 113.5 %reduce-scatter.3.cloned.1.call-start = ((), (), s32[]{:S(2)}) async-start(), calls=%async_computation.5 | async-start | bytes 921600 | tf_op jit(solution)/shard_map/reduce_scatter | solution.py:43
  201.2 184.3 %all-gather.2.cloned.1.call-start = ((), (), s32[]{:S(2)}) async-start(), calls=%async_computation.6 | async-start | bytes 16896000 | tf_op jit(solution)/shard_map/all_gather | solution.py:56
  236.2 13.0 %collective-permute-start = (bf16[1,3,200,200]{3,2,1,0:T(8,128)(2,1)S(1)}, bf16[1,3,200,200]{3,2,1,0:T(8,128)(2,1)S(1)}, u32[]{:S(2)}, u32[]{:S(2)}) collective-permute-start(bf16[1,3,200,200]{3,2,1,0:T(8,128)(2,1)S(1)} %pad_maximum_fusion.3), channel_id=1, source_target_pairs={{32,0},{64,32},{96,64},{128,96},{160,128},{192,160},{224,192},{33,... | collective-permute-start | bytes 720008 | tf_op jit(solution)/shard_map/ppermute | solution.py:50
  401.8 8.2 %copy-start.5 = (s32[256]{0:T(256)S(1)}, s32[256]{0:T(256)}, u32[]{:S(2)}) copy-start(s32[256]{0:T(256)} %param.17) | copy-start | bytes 3076
  737.1 29.2 %copy-start.1 = (s32[3072,2]{0,1:T(2,128)S(1)}, s32[3072,2]{0,1:T(2,128)}, u32[]{:S(2)}) copy-start(s32[3072,2]{0,1:T(2,128)} %param.15) | copy-start | bytes 73732
  737.8 14.2 %all-to-all-start.2 = ((f32[32,1,384]{2,1,0:T(1,128)}), f32[32,1,384]{2,1,0:T(1,128)S(1)}, u32[]{:S(2)}, u32[]{:S(2)}) async-start(f32[32,1,384]{2,1,0:T(1,128)} %broadcast_in_dim.46), calls=%async_computation.3 | async-start | bytes 98304 | tf_op jit(solution)/shard_map/all_to_all | solution.py:62
  753.9 11.8 %all-to-all-start.3 = ((f32[8,1,1]{2,1,0:T(1,128)}), f32[8,1,1]{2,1,0:T(1,128)S(1)}, u32[]{:S(2)}, u32[]{:S(2)}) async-start(f32[8,1,1]{2,1,0:T(1,128)} %broadcast_in_dim.49), calls=%async_computation.4 | async-start | bytes 8192 | tf_op jit(solution)/shard_map/all_to_all | solution.py:62
Sparse Core Ops, SparseCore 0:
  121.7 77.1 all-reduce.2
  201.5 33.5 reduce-scatter.2
  250.3 135.1 all-gather.1
